TPU v7x, 32 devices: a whole 2x2x4 slice. The times are simulated.
32 devices in a mesh: gx: 4 (over y, core), gy: 4 (over z), gz: 2 (over x).
Axes of the slice: x: 2, y: 2, z: 4, core: 2. Of those that a mesh axis runs over, the one named last changes fastest.
Arguments:
- fluid_state: float32 [6, 32, 64, 256], P(None, 'gx', 'gy', 'gz'), may hold values from -1.6 to 140, as said below
Outputs:
- new_state: float32 [6, 32, 64, 256], P(None, 'gx', 'gy', 'gz')
Inputs may be any that keep to these rules, and one draw needn't show every extreme that they name: `fluid_state`: each partial density is at least 0.05 times the density, the density lies between 0.5 and 2, and the pressure 0.4 (q5 - 0.5 times the sum over k = 0, 1, 2 of q(2+k)^2 / density) lies between 0.5 and 60.
All inputs are finite; a program needn't handle non-finite values.
Results may differ from a plain program's by a relative error of at most 0.0001.
Values sent between devices are 32-bit elements; how exact they have to be, the bound alone decides.
A program may use at most 64 MiB of HBM per device.

v0:
```python
import jax
import jax.numpy as jnp
from jax import lax
from jax.sharding import PartitionSpec as P

gamma_gas = 1.4
tension = 16.0
courant = 0.5
spacing = 0.5
weno_eps = 1e-06
normal_floor = 0.25


def padded_2(block, sides, width):
    for axis, dim in sides:
        count = lax.axis_size(axis)
        forward = [(i, i + 1) for i in range(count - 1)]
        forward.append((count - 1, 0))
        backward = [(target, source) for source, target in forward]
        low = lax.ppermute(
            lax.slice_in_dim(block, block.shape[dim] - width, None, axis=dim), axis, forward
        )
        high = lax.ppermute(lax.slice_in_dim(block, 0, width, axis=dim), axis, backward)
        block = jnp.concatenate([low, block, high], axis=dim)
    return block


def primitives(conserved):
    density = conserved[0] + conserved[1]
    velocity = conserved[2:5] / density
    kinetic = 0.5 * jnp.sum(conserved[2:5] * velocity, axis=0)
    pressure = (gamma_gas - 1.0) * (conserved[5] - kinetic)
    return (density, velocity, pressure)


def wave_speed(conserved):
    density, velocity, pressure = primitives(conserved)
    sound_speed = jnp.sqrt(gamma_gas * pressure / density)
    return jnp.max(jnp.abs(velocity), axis=0) + sound_speed


def trimmed(values, margin):
    for spatial in range(3):
        axis_pos = values.ndim - 3 + spatial
        values = lax.slice_in_dim(values, margin, values.shape[axis_pos] - margin, axis=axis_pos)
    return values


def keep_core(values, which_axis):
    for spatial in range(3):
        if spatial != which_axis:
            axis_pos = values.ndim - 3 + spatial
            values = lax.slice_in_dim(values, 3, values.shape[axis_pos] - 3, axis=axis_pos)
    return values


def derivative(source, which_axis):
    forward = source
    backward = source
    for spatial in range(3):
        axis_pos = source.ndim - 3 + spatial
        extent = source.shape[axis_pos]
        if spatial == which_axis:
            forward = lax.slice_in_dim(forward, 2, extent, axis=axis_pos)
            backward = lax.slice_in_dim(backward, 0, extent - 2, axis=axis_pos)
        else:
            forward = lax.slice_in_dim(forward, 1, extent - 1, axis=axis_pos)
            backward = lax.slice_in_dim(backward, 1, extent - 1, axis=axis_pos)
    return (forward - backward) / (2.0 * spacing)


def colour_of(conserved):
    return conserved[0] / (conserved[0] + conserved[1])


def gradient_of(colour):
    return jnp.stack([derivative(colour, 0), derivative(colour, 1), derivative(colour, 2)])


def unit_normals(gradient):
    length = jnp.sqrt(jnp.sum(gradient * gradient, axis=0))
    return gradient / jnp.maximum(length, normal_floor)


def curvature_of(normals):
    return -(derivative(normals[0], 0) + derivative(normals[1], 1) + derivative(normals[2], 2))


def weno_face(minus_two, minus_one, middle, plus_one, plus_two):
    stencil_a = (2.0 * minus_two - 7.0 * minus_one + 11.0 * middle) / 6.0
    stencil_b = (-minus_one + 5.0 * middle + 2.0 * plus_one) / 6.0
    stencil_c = (2.0 * middle + 5.0 * plus_one - plus_two) / 6.0
    smooth_a = (
        13.0 / 12.0 * (minus_two - 2.0 * minus_one + middle) ** 2
        + 0.25 * (minus_two - 4.0 * minus_one + 3.0 * middle) ** 2
    )
    smooth_b = (
        13.0 / 12.0 * (minus_one - 2.0 * middle + plus_one) ** 2
        + 0.25 * (minus_one - plus_one) ** 2
    )
    smooth_c = (
        13.0 / 12.0 * (middle - 2.0 * plus_one + plus_two) ** 2
        + 0.25 * (3.0 * middle - 4.0 * plus_one + plus_two) ** 2
    )
    weight_a = 0.1 / (weno_eps + smooth_a) ** 2
    weight_b = 0.6 / (weno_eps + smooth_b) ** 2
    weight_c = 0.3 / (weno_eps + smooth_c) ** 2
    return (weight_a * stencil_a + weight_b * stencil_b + weight_c * stencil_c) / (
        weight_a + weight_b + weight_c
    )


def flux_tendency(padded, top_speed):
    interior_shape = (6, padded.shape[1] - 6, padded.shape[2] - 6, padded.shape[3] - 6)
    tendency = jnp.zeros(interior_shape, jnp.float32)
    for which_axis in range(3):
        axis_pos = 1 + which_axis
        conserved = keep_core(padded, which_axis)
        density, velocity, pressure = primitives(conserved)
        normal_speed = velocity[which_axis]
        momenta = []
        for spatial in range(3):
            moving = conserved[2 + spatial] * normal_speed
            if spatial == which_axis:
                moving = moving + pressure
            momenta.append(moving)
        flux_whole = jnp.stack(
            [
                conserved[0] * normal_speed,
                conserved[1] * normal_speed,
                momenta[0],
                momenta[1],
                momenta[2],
                (conserved[5] + pressure) * normal_speed,
            ]
        )
        plus_part = 0.5 * (flux_whole + top_speed * conserved)
        minus_part = 0.5 * (flux_whole - top_speed * conserved)
        face_count = plus_part.shape[axis_pos] - 5

        def shifted(values, offset):
            return lax.slice_in_dim(values, 2 + offset, 2 + offset + face_count, axis=axis_pos)

        face_flux = weno_face(
            shifted(plus_part, -2),
            shifted(plus_part, -1),
            shifted(plus_part, 0),
            shifted(plus_part, 1),
            shifted(plus_part, 2),
        )
        face_flux = face_flux + weno_face(
            shifted(minus_part, 3),
            shifted(minus_part, 2),
            shifted(minus_part, 1),
            shifted(minus_part, 0),
            shifted(minus_part, -1),
        )
        upper_face = lax.slice_in_dim(face_flux, 1, face_count, axis=axis_pos)
        lower_face = lax.slice_in_dim(face_flux, 0, face_count - 1, axis=axis_pos)
        tendency = tendency - (upper_face - lower_face) / spacing
    return tendency


def capillary(interior, gradient, curvature):
    velocity = interior[2:5] / (interior[0] + interior[1])
    capillary_force = tension * curvature * gradient
    capillary_work = jnp.sum(capillary_force * velocity, axis=0)
    zero_rows = jnp.zeros((2,) + curvature.shape, jnp.float32)
    return jnp.concatenate([zero_rows, capillary_force, capillary_work[None]], axis=0)


def per_device(fluid_state):
    top_speed = lax.pmax(jnp.max(wave_speed(fluid_state)), ("gx", "gy", "gz"))
    padded = padded_2(fluid_state, (("gx", 1), ("gy", 2), ("gz", 3)), 3)
    gradient_wide = gradient_of(colour_of(trimmed(padded, 1)))
    curvature = curvature_of(unit_normals(gradient_wide))
    gradient = trimmed(gradient_wide, 1)
    timestep = courant * spacing / (3.0 * top_speed)
    tendency = flux_tendency(padded, top_speed) + capillary(fluid_state, gradient, curvature)
    return fluid_state + timestep * tendency


def solution(mesh):
    placed = (P(None, "gx", "gy", "gz"),)
    return jax.shard_map(
        per_device, mesh=mesh, in_specs=placed, out_specs=P(None, "gx", "gy", "gz"), check_vma=False
    )
```

profile of v0, /device:TPU:0, one launch (start us, length us, event | category | flops | bytes accessed | tf_op | source)
XLA Modules:
  0.0 99.7 jit_solution(366755410447460930)
XLA Ops:
  0.0 1.0 %fusion.38 = (f32[6,3,16,128]{3,2,1,0:T(8,128)S(1)}, f32[6,3,16,128]{3,2,1,0:T(8,128)S(1)}) fusion(f32[6,8,16,128]{3,2,1,0:T(8,128)} %param.1), kind=kLoop, calls=%fused_computation.117 | loop fusion | bytes 589824 | tf_op jit(solution)/shard_map/slice | solution.py:23
  1.0 0.5 collective-permute-start
  1.6 2.0 %collective-permute-start.1 = (f32[6,3,16,128]{3,2,1,0:T(8,128)S(1)}, f32[6,3,16,128]{3,2,1,0:T(8,128)S(1)}, u32[]{:S(2)}, u32[]{:S(2)}) collective-permute-start(f32[6,3,16,128]{3,2,1,0:T(8,128)S(1)} %get-tuple-element.37), channel_id=1, source_target_pairs={{8,0},{16,8},{24,16},{0,24},{9,1},{17,9},{25,17},{1,25},{10,2},{18... | collective-permute-start | bytes 442376 | tf_op jit(solution)/shard_map/ppermute | solution.py:23
  3.6 0.9 add_bitcast_fusion.3
  4.5 1.9 %collective-permute-done = f32[6,3,16,128]{3,2,1,0:T(8,128)S(1)} collective-permute-done((f32[6,3,16,128]{3,2,1,0:T(8,128)S(1)}, f32[6,3,16,128]{3,2,1,0:T(8,128)S(1)}, u32[]{:S(2)}, u32[]{:S(2)}) %collective-permute-start) | collective-permute-done | bytes 147488 | tf_op jit(solution)/shard_map/ppermute | solution.py:20
  6.3 1.0 %constant_dynamic-update-slice_fusion.1 = f32[6,14,16,128]{3,2,1,0:T(8,128)S(1)} fusion(f32[6,14,16,128]{3,2,1,0:T(8,128)S(1)} %constant_dynamic-update-slice_fusion.2, f32[6,8,16,128]{3,2,1,0:T(8,128)} %param.1), kind=kLoop, calls=%fused_computation.113 | loop fusion | bytes 786432
  7.4 0.4 collective-permute-done.1
  7.7 0.1 fusion.37
  7.9 4.1 %collective-permute-start.3 = (f32[6,14,3,128]{3,1,2,0:T(8,128)S(1)}, f32[6,14,3,128]{3,1,2,0:T(8,128)S(1)}, u32[]{:S(2)}, u32[]{:S(2)}) collective-permute-start(f32[6,14,3,128]{3,1,2,0:T(8,128)S(1)} %copy.119), channel_id=1, source_target_pairs={{2,0},{4,2},{6,4},{0,6},{3,1},{5,3},{7,5},{1,7},{10,8},{12,10},{14... | collective-permute-start | bytes 387080 | tf_op jit(solution)/shard_map/ppermute | solution.py:23
  12.3 4.0 %collective-permute-done.3 = f32[6,14,3,128]{3,1,2,0:T(8,128)S(1)} collective-permute-done((f32[6,14,3,128]{3,1,2,0:T(8,128)S(1)}, f32[6,14,3,128]{3,1,2,0:T(8,128)S(1)}, u32[]{:S(2)}, u32[]{:S(2)}) %collective-permute-start.3) | collective-permute-done | bytes 129056 | tf_op jit(solution)/shard_map/ppermute | solution.py:23
  16.2 0.1 copy.109
  16.3 3.6 %collective-permute-done.2 = f32[6,14,3,128]{3,1,2,0:T(8,128)S(1)} collective-permute-done((f32[6,14,3,128]{3,1,2,0:T(8,128)S(1)}, f32[6,14,3,128]{3,1,2,0:T(8,128)S(1)}, u32[]{:S(2)}, u32[]{:S(2)}) %collective-permute-start.2) | collective-permute-done | bytes 129056 | tf_op jit(solution)/shard_map/ppermute | solution.py:20
  19.9 0.1 copy.108
  19.9 0.2 pad_maximum_fusion.1
  20.2 1.3 %fusion.36 = (f32[6,14,22,3]{3,2,1,0:T(8,128)S(1)}, f32[6,14,22,3]{3,2,1,0:T(8,128)}) fusion(f32[6,14,22,128]{3,2,1,0:T(8,128)S(1)} %pad_maximum_fusion.1), kind=kLoop, calls=%fused_computation.115 | loop fusion | bytes 88704 | tf_op jit(solution)/shard_map/slice | solution.py:21
  21.5 2.6 %copy.113 = f32[6,14,22,3]{2,1,3,0:T(8,128)} copy(f32[6,14,22,3]{3,2,1,0:T(8,128)} %get-tuple-element.28) | data formatting | bytes 44352 | tf_op jit(solution)/shard_map/slice | solution.py:23
  24.0 1.5 %collective-permute-start.5 = (f32[6,14,22,3]{2,1,3,0:T(8,128)}, f32[6,14,22,3]{2,1,3,0:T(8,128)}, u32[]{:S(2)}, u32[]{:S(2)}) collective-permute-start(f32[6,14,22,3]{2,1,3,0:T(8,128)} %copy.113), channel_id=1, source_target_pairs={{1,0},{0,1},{3,2},{2,3},{5,4},{4,5},{7,6},{6,7},{9,8},{8,9},{11,10... | collective-permute-start | bytes 66536 | tf_op jit(solution)/shard_map/ppermute | solution.py:23
  25.5 1.4 %copy.112 = f32[6,14,22,3]{2,1,3,0:T(8,128)} copy(f32[6,14,22,3]{3,2,1,0:T(8,128)S(1)} %get-tuple-element.27) | data formatting | bytes 44352 | tf_op jit(solution)/shard_map/slice | solution.py:21
  26.9 0.5 collective-permute-start.4
  27.7 2.4 %collective-permute-done.5 = f32[6,14,22,3]{2,1,3,0:T(8,128)} collective-permute-done((f32[6,14,22,3]{2,1,3,0:T(8,128)}, f32[6,14,22,3]{2,1,3,0:T(8,128)}, u32[]{:S(2)}, u32[]{:S(2)}) %collective-permute-start.5) | collective-permute-done | bytes 22208 | tf_op jit(solution)/shard_map/ppermute | solution.py:23
  30.1 1.5 %copy.115 = f32[6,14,22,3]{3,2,1,0:T(8,128)S(1)} copy(f32[6,14,22,3]{2,1,3,0:T(8,128)} %collective-permute-done.5) | data formatting | bytes 44352 | tf_op jit(solution)/shard_map/ppermute | solution.py:23
  31.7 1.1 %collective-permute-done.4 = f32[6,14,22,3]{2,1,3,0:T(8,128)} collective-permute-done((f32[6,14,22,3]{2,1,3,0:T(8,128)}, f32[6,14,22,3]{2,1,3,0:T(8,128)}, u32[]{:S(2)}, u32[]{:S(2)}) %collective-permute-start.4) | collective-permute-done | bytes 22208 | tf_op jit(solution)/shard_map/ppermute | solution.py:20
  32.7 1.5 %copy.114 = f32[6,14,22,3]{3,2,1,0:T(8,128)S(1)} copy(f32[6,14,22,3]{2,1,3,0:T(8,128)} %collective-permute-done.4) | data formatting | bytes 44352 | tf_op jit(solution)/shard_map/ppermute | solution.py:20
  34.2 0.2 add_bitcast_fusion
  34.5 1.2 %pad_maximum_fusion = f32[6,14,22,134]{3,2,1,0:T(8,128)S(1)} fusion(f32[6,14,22,3]{3,2,1,0:T(8,128)S(1)} %copy.115, f32[6,14,3,128]{3,2,1,0:T(4,128)S(1)} %copy.109, f32[6,14,16,128]{3,2,1,0:T(8,128)S(1)} %constant_dynamic-update-slice_fusion, f32[6,14,3,128]{3,2,1,0:T(4,128)S(1)} %copy.108, f32[6,14,22,3]{3,2,1,0:T(8,128)S(1)} %copy.114), kind=kLoop, calls=%fused_computation | loop fusion | flops 990528 | bytes 1981056 | tf_op jit(solution)/shard_map/concatenate | solution.py:24
  35.7 0.5 add_divide_fusion
  36.2 0.1 multiply_reduce_fusion.1
  36.3 0.8 multiply_dynamic-update-slice_fusion.2
  37.1 0.7 multiply_dynamic-update-slice_fusion.1
  37.7 0.8 fusion.15
  38.5 0.8 fusion.14
  39.3 0.4 fusion.11
  39.7 0.1 multiply_reduce_fusion
  39.8 0.1 sqrt_maximum_fusion
  39.9 0.1 broadcast_divide_fusion
  40.1 0.9 fusion.13
  41.0 0.2 fusion.29
  41.1 0.8 multiply_reduce_fusion.4
  41.9 0.6 fusion.35
  42.6 0.8 multiply_dynamic-update-slice_fusion
  43.4 39.9 %pmax.7 = f32[]{:T(128)} all-reduce(f32[]{:T(128)} %fusion.35), channel_id=1, replica_groups=mesh['gx'=4,'gy'=4,'gz'=2] {'gx','gy','gz'}, use_global_device_ids=true, to_apply=%region_3.0 | all-reduce | flops 1 | bytes 8 | tf_op jit(solution)/shard_map/pmax | solution.py:173
  83.2 2.5 %add_multiply_fusion = (f32[6,8,16,134]{3,2,1,0:T(8,128)S(1)}, f32[6,8,16,134]{3,2,1,0:T(8,128)S(1)}) fusion(f32[6,8,16,134]{3,2,1,0:T(8,128)} %multiply_dynamic-update-slice_fusion, f32[6,14,22,134]{3,2,1,0:T(8,128)} %copy-done.6, f32[]{:T(128)} %pmax.7), kind=kLoop, calls=%fused_computation.5 | loop fusion | flops 514560 | bytes 1646596 | tf_op jit(solution)/shard_map/mul | solution.py:137
  85.8 0.7 add_multiply_fusion.2
  86.5 1.8 %add_multiply_fusion.1 = (f32[6,14,16,128]{3,2,1,0:T(8,128)}, f32[6,14,16,128]{3,2,1,0:T(8,128)}) fusion(f32[6,14,16,128]{3,2,1,0:T(8,128)S(1)} %copy-done.9, f32[6,14,16,128]{3,2,1,0:T(8,128)S(1)} %constant_dynamic-update-slice_fusion, f32[]{:T(128)} %pmax.7), kind=kLoop, calls=%fused_computation.9 | loop fusion | flops 860160 | bytes 2752516 | tf_op jit(solution)/shard_map/mul | solution.py:137
  88.9 4.7 %divide_add_fusion = f32[6,8,16,129]{3,2,1,0:T(8,128)} fusion(f32[6,8,16,134]{3,2,1,0:T(8,128)S(1)} %get-tuple-element.22, f32[6,8,16,134]{3,2,1,0:T(8,128)S(1)} %get-tuple-element.21), kind=kLoop, calls=%fused_computation.3 | loop fusion | flops 12780288 | bytes 4359168 | tf_op jit(solution)/shard_map/add | solution.py:151
  93.6 3.0 %divide_add_fusion.1 = f32[6,8,17,128]{3,2,1,0:T(8,128)S(1)} fusion(f32[6,8,22,128]{3,2,1,0:T(8,128)S(1)} %get-tuple-element.24, f32[6,8,22,128]{3,2,1,0:T(8,128)S(1)} %get-tuple-element.23), kind=kLoop, calls=%fused_computation.11 | loop fusion | flops 13473792 | bytes 4595712 | tf_op jit(solution)/shard_map/add | solution.py:151
  96.7 2.0 %divide_add_fusion.2 = f32[6,9,16,128]{3,2,1,0:T(8,128)S(1)} fusion(f32[6,14,16,128]{3,2,1,0:T(8,128)S(1)} %copy-done.3, f32[6,14,16,128]{3,2,1,0:T(8,128)S(1)} %copy-done.2), kind=kLoop, calls=%fused_computation.14 | loop fusion | flops 14266368 | bytes 4866048 | tf_op jit(solution)/shard_map/add | solution.py:151
  98.8 1.0 fusion.4
  (50 shorter events, 0.7 us)
Async XLA Ops:
  1.0 5.3 %collective-permute-start = (f32[6,3,16,128]{3,2,1,0:T(8,128)S(1)}, f32[6,3,16,128]{3,2,1,0:T(8,128)S(1)}, u32[]{:S(2)}, u32[]{:S(2)}) collective-permute-start(f32[6,3,16,128]{3,2,1,0:T(8,128)S(1)} %get-tuple-element.38), channel_id=1, source_target_pairs={{0,8},{8,16},{16,24},{24,0},{1,9},{9,17},{17,25},{25,1},{2,10},{10... | collective-permute-start | bytes 442376 | tf_op jit(solution)/shard_map/ppermute | solution.py:20
  1.6 6.2 %collective-permute-start.1 = (f32[6,3,16,128]{3,2,1,0:T(8,128)S(1)}, f32[6,3,16,128]{3,2,1,0:T(8,128)S(1)}, u32[]{:S(2)}, u32[]{:S(2)}) collective-permute-start(f32[6,3,16,128]{3,2,1,0:T(8,128)S(1)} %get-tuple-element.37), channel_id=1, source_target_pairs={{8,0},{16,8},{24,16},{0,24},{9,1},{17,9},{25,17},{1,25},{10,2},{18... | collective-permute-start | bytes 442376 | tf_op jit(solution)/shard_map/ppermute | solution.py:23
  7.9 8.4 %collective-permute-start.3 = (f32[6,14,3,128]{3,1,2,0:T(8,128)S(1)}, f32[6,14,3,128]{3,1,2,0:T(8,128)S(1)}, u32[]{:S(2)}, u32[]{:S(2)}) collective-permute-start(f32[6,14,3,128]{3,1,2,0:T(8,128)S(1)} %copy.119), channel_id=1, source_target_pairs={{2,0},{4,2},{6,4},{0,6},{3,1},{5,3},{7,5},{1,7},{10,8},{12,10},{14... | collective-permute-start | bytes 387080 | tf_op jit(solution)/shard_map/ppermute | solution.py:23
  12.0 7.9 %collective-permute-start.2 = (f32[6,14,3,128]{3,1,2,0:T(8,128)S(1)}, f32[6,14,3,128]{3,1,2,0:T(8,128)S(1)}, u32[]{:S(2)}, u32[]{:S(2)}) collective-permute-start(f32[6,14,3,128]{3,1,2,0:T(8,128)S(1)} %copy.118), channel_id=1, source_target_pairs={{0,2},{2,4},{4,6},{6,0},{1,3},{3,5},{5,7},{7,1},{8,10},{10,12},{12... | collective-permute-start | bytes 387080 | tf_op jit(solution)/shard_map/ppermute | solution.py:20
  12.3 7.6 %copy-start.8 = (f32[6,14,16,128]{3,2,1,0:T(8,128)}, f32[6,14,16,128]{3,2,1,0:T(8,128)S(1)}, u32[]{:S(2)}) copy-start(f32[6,14,16,128]{3,2,1,0:T(8,128)S(1)} %multiply_dynamic-update-slice_fusion.3) | copy-start | bytes 2064388
  20.1 7.3 %copy-start = (f32[6,14,22,128]{3,2,1,0:T(8,128)}, f32[6,14,22,128]{3,2,1,0:T(8,128)S(1)}, u32[]{:S(2)}) copy-start(f32[6,14,22,128]{3,2,1,0:T(8,128)S(1)} %pad_maximum_fusion.1) | copy-start | bytes 2838532
  24.0 6.1 %collective-permute-start.5 = (f32[6,14,22,3]{2,1,3,0:T(8,128)}, f32[6,14,22,3]{2,1,3,0:T(8,128)}, u32[]{:S(2)}, u32[]{:S(2)}) collective-permute-start(f32[6,14,22,3]{2,1,3,0:T(8,128)} %copy.113), channel_id=1, source_target_pairs={{1,0},{0,1},{3,2},{2,3},{5,4},{4,5},{7,6},{6,7},{9,8},{8,9},{11,10... | collective-permute-start | bytes 66536 | tf_op jit(solution)/shard_map/ppermute | solution.py:23
  26.9 5.8 %collective-permute-start.4 = (f32[6,14,22,3]{2,1,3,0:T(8,128)}, f32[6,14,22,3]{2,1,3,0:T(8,128)}, u32[]{:S(2)}, u32[]{:S(2)}) collective-permute-start(f32[6,14,22,3]{2,1,3,0:T(8,128)} %copy.112), channel_id=1, source_target_pairs={{0,1},{1,0},{2,3},{3,2},{4,5},{5,4},{6,7},{7,6},{8,9},{9,8},{10,11... | collective-permute-start | bytes 66536 | tf_op jit(solution)/shard_map/ppermute | solution.py:20
  27.7 3.9 %copy-start.10 = (f32[6,8,22,128]{3,2,1,0:T(8,128)}, f32[6,8,22,128]{3,2,1,0:T(8,128)S(1)}, u32[]{:S(2)}) copy-start(f32[6,8,22,128]{3,2,1,0:T(8,128)S(1)} %multiply_dynamic-update-slice_fusion.6) | copy-start | bytes 1622020
  35.7 4.0 %copy-start.6 = (f32[6,14,22,134]{3,2,1,0:T(8,128)}, f32[6,14,22,134]{3,2,1,0:T(8,128)S(1)}, u32[]{:S(2)}) copy-start(f32[6,14,22,134]{3,2,1,0:T(8,128)S(1)} %pad_maximum_fusion) | copy-start | bytes 2971588
  40.1 1.0 %copy-start.4 = (f32[6,8,16,128]{3,2,1,0:T(8,128)S(1)}, f32[6,8,16,128]{3,2,1,0:T(8,128)}, u32[]{:S(2)}) copy-start(f32[6,8,16,128]{3,2,1,0:T(8,128)} %param.1) | copy-start | bytes 1179652
  83.2 2.5 %copy-start.1 = (f32[6,14,22,128]{3,2,1,0:T(8,128)S(1)}, f32[6,14,22,128]{3,2,1,0:T(8,128)}, u32[]{:S(2)}) copy-start(f32[6,14,22,128]{3,2,1,0:T(8,128)} %copy-done) | copy-start | bytes 2838532
  83.2 2.6 %copy-start.11 = (f32[6,8,22,128]{3,2,1,0:T(8,128)S(1)}, f32[6,8,22,128]{3,2,1,0:T(8,128)}, u32[]{:S(2)}) copy-start(f32[6,8,22,128]{3,2,1,0:T(8,128)} %copy-done.10) | copy-start | bytes 1622020
  83.2 3.3 %copy-start.9 = (f32[6,14,16,128]{3,2,1,0:T(8,128)S(1)}, f32[6,14,16,128]{3,2,1,0:T(8,128)}, u32[]{:S(2)}) copy-start(f32[6,14,16,128]{3,2,1,0:T(8,128)} %copy-done.8) | copy-start | bytes 2064388
  93.6 3.0 %copy-start.2 = (f32[6,14,16,128]{3,2,1,0:T(8,128)S(1)}, f32[6,14,16,128]{3,2,1,0:T(8,128)}, u32[]{:S(2)}) copy-start(f32[6,14,16,128]{3,2,1,0:T(8,128)} %get-tuple-element.25) | copy-start | bytes 2064388
  93.6 3.0 %copy-start.3 = (f32[6,14,16,128]{3,2,1,0:T(8,128)S(1)}, f32[6,14,16,128]{3,2,1,0:T(8,128)}, u32[]{:S(2)}) copy-start(f32[6,14,16,128]{3,2,1,0:T(8,128)} %get-tuple-element.26) | copy-start | bytes 2064388
  96.6 2.1 %copy-start.5 = (f32[6,8,16,128]{3,2,1,0:T(8,128)S(1)}, f32[6,8,16,128]{3,2,1,0:T(8,128)}, u32[]{:S(2)}) copy-start(f32[6,8,16,128]{3,2,1,0:T(8,128)} %param.1) | copy-start | bytes 1179652
  96.6 2.1 %copy-start.7 = (f32[6,8,16,129]{3,2,1,0:T(8,128)S(1)}, f32[6,8,16,129]{3,2,1,0:T(8,128)}, u32[]{:S(2)}) copy-start(f32[6,8,16,129]{3,2,1,0:T(8,128)} %divide_add_fusion) | copy-start | bytes 1188868
  96.7 2.1 %copy-start.12 = (f32[3,8,16,128]{3,2,1,0:T(8,128)S(1)}, f32[3,8,16,128]{3,2,1,0:T(8,128)}, u32[]{:S(2)}) copy-start(f32[3,8,16,128]{3,2,1,0:T(8,128)} %get-tuple-element.15) | copy-start | bytes 589828
where the time goes:
time: 100 us; the launch traced here: 99.7 us
  blocking collectives  39.9 us (40%)
  other arithmetic  26.2 us (26%)
  waiting for transfers between devices  13.2 us (13%)
  local copies, waits for them, and re-layouts  10.7 us (11%)
  starting transfers between devices  8.74 us (9%)
  between operations  1.02 us (1%)
    pmax x1, blocking collectives, per_device(): top_speed = lax.pmax(jnp.max(wave_speed(fluid_state)), ('gx', 'gy', 'gz'))  39.9 us
    add x3, other arithmetic, flux_tendency(): face_flux + weno_face(shifted(minus_part, 3), shifted(minus_part, 2), shi...  9.67 us
    ppermute x3, starting transfers between devices, padded_2(): lax.ppermute(lax.slice_in_dim(block, 0, width, axis=dim), axis, backward)  7.6 us
    ppermute x3, waiting for transfers between devices, padded_2(): lax.ppermute(lax.slice_in_dim(block, 0, width, axis=dim), axis, backward)  6.71 us
    ppermute x3, waiting for transfers between devices, padded_2(): lax.ppermute(lax.slice_in_dim(block, block.shape[dim] - width, None, axis...  6.49 us
    mul x3, other arithmetic, flux_tendency(): plus_part = 0.5 * (flux_whole + top_speed * conserved)  5.07 us
    unnamed x15, other arithmetic  4.11 us
    slice x2, local copies, waits for them, and re-layouts, padded_2(): lax.slice_in_dim(block, 0, width, axis=dim)  3.59 us
  transfers between devices with their start and end apart: 6, of which 6 were waited for; matrix products, arithmetic and copies ran while one was open for 5% of the time, Pallas kernels for 0%

commit v1 on v0

v1 whole, which is shorter than its diff:
```python
import functools

import jax
import jax.numpy as jnp
from jax import lax
from jax.experimental import pallas as pl
from jax.experimental.pallas import tpu as pltpu
from jax.sharding import PartitionSpec as P

gamma_gas = 1.4
tension = 16.0
courant = 0.5
spacing = 0.5
weno_eps = 1e-06
normal_floor = 0.25

MESH = pl.DeviceIdType.MESH
SUB, LANES = 8, 128
SCALE = 0.25
F32 = jnp.float32


def primitives(q):
    inverse = 1.0 / (q[0] + q[1])
    u = [q[2 + k] * inverse for k in range(3)]
    kinetic = 0.5 * (q[2] * u[0] + q[3] * u[1] + q[4] * u[2])
    return inverse, u, (gamma_gas - 1.0) * (q[5] - kinetic)


def scaled_flux(q, k):
    _, u, p = primitives(q)
    speed = (0.5 * SCALE) * u[k]
    out = [q[c] * speed for c in range(5)] + [(q[5] + p) * speed]
    out[2 + k] = out[2 + k] + (0.5 * SCALE) * p
    return out


def correction(e0, e1, e2, third_a, third_b):
    q0, q1, q2 = e0 * e0, e1 * e1, e2 * e2
    a = q1 * q2
    b = 3.0 * (q0 * q1)
    total = a + (b + 6.0 * (q0 * q2))
    return (a * third_a + b * third_b) / total


def differences(v):
    n = len(v)
    d = [v[i + 1] - v[i] for i in range(n - 1)]
    h = [None] + [0.5 * (d[i] - d[i - 1]) for i in range(1, n - 1)]
    e = [None] + [h[i] * h[i] * (13.0 / 3.0) + weno_eps * SCALE * SCALE for i in range(1, n - 1)]
    j = [None, None] + [(2.0 / 3.0) * (h[i] - h[i - 1]) for i in range(2, n - 1)]
    return d, h, e, j


def square(value):
    return value * value


def weno_tendency(flux, state):
    n = len(flux)
    vp = [f + s for f, s in zip(flux, state)]
    vm = [f - s for f, s in zip(flux, state)]
    d, h, e, j = differences(vp)
    dm, hm, em, jm = differences(vm)
    faces = []
    for i in range(2, n - 3):
        fix = correction(
            e[i - 1] + square(d[i - 1] + h[i - 1]),
            e[i] + square(d[i - 1] + h[i]),
            e[i + 1] + square(h[i + 1] - d[i]),
            j[i],
            0.5 * j[i + 1],
        )
        fix_m = correction(
            em[i + 2] + square(hm[i + 2] - dm[i + 1]),
            em[i + 1] + square(hm[i + 1] - dm[i + 1]),
            em[i] + square(hm[i] + dm[i]),
            jm[i + 2],
            0.5 * jm[i + 1],
        )
        linear = (vp[i] + vm[i + 1]) + 0.5 * (d[i - 1] - dm[i + 1]) + (2.0 / 3.0) * (h[i] + hm[i + 1])
        faces.append(linear + (fix_m - fix))
    return [faces[i + 1] - faces[i] for i in range(len(faces) - 1)]


def kernel(sizes, q_hbm, out_ref, px, py, pz, fx, fy, fz, tq, zsend, zleft, zright, ts0, ts1, tsa, tsb, speed_ref,
           gb, nb, tb, nxp, nyp, nzp, nzsend, nzleft, nzright, src, ay, tz,
           local_sem, send_sem, recv_sem, sa_sem, ra_sem, sb_sem, rb_sem):
    ngx, ngy, ngz = sizes
    X, Y, Z = px.shape[1] - 6, px.shape[2], px.shape[3]
    step = Z // SUB
    lines = X * Y
    ix, iy, iz = lax.axis_index("gx"), lax.axis_index("gy"), lax.axis_index("gz")
    offsets_b = [(a, b) for a in range(ngy) for b in range(ngz) if (a, b) != (0, 0)]

    load = pltpu.make_async_copy(q_hbm, px.at[:, 3 : 3 + X], local_sem)
    load.start()
    barrier = pltpu.get_barrier_semaphore()

    def peer_x(offset):
        return {"gx": lax.rem(ix + offset + ngx, ngx)}

    def peer_yz(a, b):
        return {"gy": lax.rem(iy + a + ngy, ngy), "gz": lax.rem(iz + b + ngz, ngz)}

    for offset in range(1, ngx):
        pl.semaphore_signal(barrier, inc=1, device_id=peer_x(offset), device_id_type=MESH)
    for a, b in offsets_b:
        pl.semaphore_signal(barrier, inc=1, device_id=peer_yz(a, b), device_id_type=MESH)

    row = lax.broadcasted_iota(jnp.int32, (SUB, LANES), 0)
    pxf = px.reshape(6 * (X + 6) * Y, LANES)
    tqf = tq.reshape(6 * Z, lines)
    halves = Y // SUB

    def rows_y(base, y):
        return pl.ds(base + y, SUB, stride=Y)

    def rows_z(base, b):
        return pl.ds(base + b, SUB, stride=step)

    load.wait()
    best = None
    for x in range(X):
        for half in range(halves):
            q = [px[c, 3 + x, half * SUB : (half + 1) * SUB, :] for c in range(6)]
            inverse, u, p = primitives(q)
            top = jnp.maximum(jnp.maximum(jnp.abs(u[0]), jnp.abs(u[1])), jnp.abs(u[2]))
            top = top + jnp.sqrt(gamma_gas * p * inverse)
            best = top if best is None else jnp.maximum(best, top)
    ts0[...] = best

    def lay_out(c, carry):
        for y in range(Y):
            py[c, 3 + y] = pxf[rows_y((c * (X + 6) + 3) * Y, y), :]
        turned = px[c, 3 : 3 + X].reshape(lines, Z).T
        tq[c] = turned
        zsend[c] = jnp.where(row < 4, turned[:SUB], turned[Z - SUB :])
        return carry

    lax.fori_loop(0, 6, lay_out, 0)
    pl.semaphore_wait(barrier, ngx - 1 + len(offsets_b))

    def remote(source, target, index, peer, sends=send_sem, recvs=recv_sem):
        copy = pltpu.make_async_remote_copy(
            src_ref=source, dst_ref=target, send_sem=sends.at[index], recv_sem=recvs.at[index],
            device_id=peer, device_id_type=MESH,
        )
        copy.start()
        return copy

    reduce_a = [remote(ts0, tsa.at[o - 1], o - 1, peer_x(o), sa_sem, ra_sem) for o in range(1, ngx)]
    xlow, xhigh, ilow, ihigh = pl.ds(0, 3), pl.ds(3 + X, 3), pl.ds(3, 3), pl.ds(X, 3)
    first, rest = pl.ds(0, 2), pl.ds(2, 4)
    halo_x0 = [
        remote(px.at[first, ihigh], px.at[first, xlow], 0, peer_x(1)),
        remote(px.at[first, ilow], px.at[first, xhigh], 1, peer_x(-1)),
    ]
    halo_z = [remote(zsend, zleft, 2, peer_yz(0, 1))]
    if ngz > 2:
        halo_z.append(remote(zsend, zright, 3, peer_yz(0, -1)))
        from_right = zright
    else:
        from_right = zleft
    halo_y = [
        remote(py.at[:, pl.ds(Y, 3)], py.at[:, pl.ds(0, 3)], 4, peer_yz(1, 0)),
        remote(py.at[:, pl.ds(3, 3)], py.at[:, pl.ds(3 + Y, 3)], 5, peer_yz(-1, 0)),
    ]
    halo_x1 = [
        remote(px.at[rest, ihigh], px.at[rest, xlow], 6, peer_x(1)),
        remote(px.at[rest, ilow], px.at[rest, xhigh], 7, peer_x(-1)),
    ]

    def fill_z(c, carry):
        for b in range(step):
            pz[c, 3 + b] = tqf[rows_z(c * Z, b), :]
        return carry

    lax.fori_loop(0, 6, fill_z, 0)

    def flux_x(at):
        for half in range(halves):
            part = pl.ds(half * SUB, SUB)
            values = scaled_flux([px[c, at, part, :] for c in range(6)], 0)
            for c in range(6):
                fx[c, at, part, :] = values[c]

    def flux_of(padded, target, k, at):
        values = scaled_flux([padded[c, at] for c in range(6)], k)
        for c in range(6):
            target[c, at] = values[c]

    def inner_x(t, carry):
        flux_x(3 + 2 * t)
        flux_x(4 + 2 * t)
        return carry

    def inner_yz(t, carry):
        for extra in range(2):
            flux_of(py, fy, 1, 3 + 2 * t + extra)
            flux_of(pz, fz, 2, 3 + 2 * t + extra)
        return carry

    lax.fori_loop(0, X // 2, inner_x, 0)

    for copy in reduce_a:
        copy.wait()
    best = ts0[...]
    for o in range(ngx - 1):
        best = jnp.maximum(best, tsa[o])
    ts1[...] = best

    lax.fori_loop(0, Y // 2, inner_yz, 0)
    reduce_b = [
        remote(ts1, tsb.at[o], o, peer_yz(*offsets_b[o]), sb_sem, rb_sem) for o in range(len(offsets_b))
    ]

    def colour(q0, q1):
        return q0 / (q0 + q1)

    central = 1.0 / (2.0 * spacing)
    for copy in halo_z:
        copy.wait()

    def join_z(c, carry):
        for s in range(3):
            low = pltpu.roll(pz[c, step + s], 1, 0)
            left = jnp.broadcast_to(zleft[c, pl.ds(5 + s, 1), :], (SUB, LANES))
            pz[c, s] = jnp.where(row == 0, left, low)
            high = pltpu.roll(pz[c, 3 + s], SUB - 1, 0)
            right = jnp.broadcast_to(from_right[c, pl.ds(s, 1), :], (SUB, LANES))
            pz[c, 3 + step + s] = jnp.where(row == SUB - 1, right, high)
        return carry

    lax.fori_loop(0, 6, join_z, 0)
    colours = [colour(pz[0, 2 + b], pz[1, 2 + b]) for b in range(step + 2)]
    for b in range(step):
        tb[rows_z(0, b), :] = (colours[b + 2] - colours[b]) * central
    gb[2] = tb[...].T
    for s in range(3):
        flux_of(pz, fz, 2, s)
        flux_of(pz, fz, 2, 3 + step + s)

    for copy in halo_y:
        copy.wait()
    colours = [colour(py[0, 2 + y], py[1, 2 + y]) for y in range(Y + 2)]
    gbf = gb.reshape(3 * lines, LANES)
    for y in range(Y):
        gbf[rows_y(lines, y), :] = (colours[y + 2] - colours[y]) * central

    for copy in halo_x0:
        copy.wait()
    for half in range(halves):
        part = pl.ds(half * SUB, SUB)
        colours = [colour(px[0, 2 + x, part, :], px[1, 2 + x, part, :]) for x in range(X + 2)]
        for x in range(X):
            at = pl.ds(x * Y + half * SUB, SUB)
            g = [(colours[x + 2] - colours[x]) * central, gb[1, at, :], gb[2, at, :]]
            gb[0, at, :] = g[0]
            length = jnp.sqrt(g[0] * g[0] + g[1] * g[1] + g[2] * g[2])
            inverse = 1.0 / jnp.maximum(length, normal_floor)
            nxp[1 + x, part, :] = g[0] * inverse
            nb[0, at, :] = g[1] * inverse
            nb[1, at, :] = g[2] * inverse
    nbf = nb.reshape(2 * lines, LANES)
    tb[...] = nb[1].T
    nzsend[...] = jnp.where(row < 4, tb[:SUB, :], tb[Z - SUB :, :])
    for y in range(Y):
        nyp[1 + y] = nbf[rows_y(0, y), :]
    for b in range(step):
        nzp[1 + b] = tb[rows_z(0, b), :]
    normals = [
        remote(nxp.at[pl.ds(X, 1)], nxp.at[pl.ds(0, 1)], 8, peer_x(1)),
        remote(nxp.at[pl.ds(1, 1)], nxp.at[pl.ds(1 + X, 1)], 9, peer_x(-1)),
        remote(nyp.at[pl.ds(Y, 1)], nyp.at[pl.ds(0, 1)], 10, peer_yz(1, 0)),
        remote(nyp.at[pl.ds(1, 1)], nyp.at[pl.ds(1 + Y, 1)], 11, peer_yz(-1, 0)),
        remote(nzsend, nzleft, 12, peer_yz(0, 1)),
    ]
    if ngz > 2:
        normals.append(remote(nzsend, nzright, 13, peer_yz(0, -1)))
        normal_right = nzright
    else:
        normal_right = nzleft
    for s in range(3):
        flux_of(py, fy, 1, s)
        flux_of(py, fy, 1, 3 + Y + s)

    for copy in reduce_b:
        copy.wait()
    best = ts1[...]
    for o in range(len(offsets_b)):
        best = jnp.maximum(best, tsb[o])
    best = jnp.max(jnp.max(best, axis=1, keepdims=True), axis=0, keepdims=True)
    speed_ref[...] = jnp.broadcast_to(best, (SUB, LANES))

    def sweep_z(c, carry):
        scaled = (0.5 * SCALE) * speed_ref[...]
        count = step + 6
        parts = weno_tendency([fz[c, s] for s in range(count)], [pz[c, s] * scaled for s in range(count)])
        tzf = tz.reshape(6 * Z, lines)
        for b in range(step):
            tzf[rows_z(c * Z, b), :] = parts[b]
        return carry

    def sweep_y(c, carry):
        scaled = (0.5 * SCALE) * speed_ref[...]
        count = Y + 6
        parts = weno_tendency([fy[c, s] for s in range(count)], [py[c, s] * scaled for s in range(count)])
        ayf = ay.reshape(6 * lines, LANES)
        for y in range(Y):
            ayf[rows_y(c * lines, y), :] = parts[y]
        return carry

    lax.fori_loop(0, 6, sweep_z, 0)
    lax.fori_loop(0, 6, sweep_y, 0)

    for copy in normals:
        copy.wait()
    left = jnp.broadcast_to(nzleft[pl.ds(SUB - 1, 1), :], (SUB, LANES))
    nzp[0] = jnp.where(row == 0, left, pltpu.roll(nzp[step], 1, 0))
    right = jnp.broadcast_to(normal_right[pl.ds(0, 1), :], (SUB, LANES))
    nzp[1 + step] = jnp.where(row == SUB - 1, right, pltpu.roll(nzp[1], SUB - 1, 0))
    for b in range(step):
        tb[rows_z(0, b), :] = nzp[b + 2] - nzp[b]
    nb[1] = tb[...].T
    for y in range(Y):
        nbf[rows_y(0, y), :] = nyp[y + 2] - nyp[y]
    zero = jnp.zeros((SUB, LANES), F32)
    for x in range(X):
        for half in range(halves):
            part = pl.ds(half * SUB, SUB)
            at = pl.ds(x * Y + half * SUB, SUB)
            q = [px[c, 3 + x, part, :] for c in range(5)]
            inverse = 1.0 / (q[0] + q[1])
            along = (nxp[x + 2, part, :] - nxp[x, part, :]) + nb[0, at, :] + nb[1, at, :]
            pull = (-tension * central) * along
            force = [pull * gb[k, at, :] for k in range(3)]
            src[0, at, :] = zero
            src[1, at, :] = zero
            for k in range(3):
                src[2 + k, at, :] = force[k]
            src[5, at, :] = (force[0] * q[2] + force[1] * q[3] + force[2] * q[4]) * inverse

    for copy in halo_x1:
        copy.wait()
    for s in range(3):
        flux_x(s)
        flux_x(3 + X + s)

    def sweep_x(c, carry):
        top = speed_ref[...]
        scaled = (0.5 * SCALE) * top
        timestep = (courant * spacing) / (3.0 * top)
        slope = timestep * (-1.0 / (spacing * SCALE))
        count = X + 6
        back = tz[c].T
        for half in range(halves):
            part = pl.ds(half * SUB, SUB)
            state = [px[c, s, part, :] for s in range(count)]
            parts = weno_tendency([fx[c, s, part, :] for s in range(count)], [v * scaled for v in state])
            for x in range(X):
                start = x * Y + half * SUB
                at = pl.ds(start, SUB)
                change = parts[x] + ay[c, at, :] + back[start : start + SUB]
                out_ref[c, x, part, :] = state[3 + x] + (slope * change + timestep * src[c, at, :])
        return carry

    lax.fori_loop(0, 6, sweep_x, 0)


def solution(mesh):
    sizes = tuple(mesh.shape[name] for name in ("gx", "gy", "gz"))
    others = sizes[1] * sizes[2] - 1

    def per_device(q):
        _, X, Y, Z = q.shape
        step = Z // SUB
        lines = X * Y
        assert X == SUB and Y % SUB == 0 and Z == LANES and lines == LANES and min(sizes) > 1

        def vmem(*shape):
            return pltpu.VMEM(shape, F32)

        dma = pltpu.SemaphoreType.DMA
        return pl.pallas_call(
            functools.partial(kernel, sizes),
            name="section",
            out_shape=jax.ShapeDtypeStruct(q.shape, F32),
            in_specs=[pl.BlockSpec(memory_space=pl.ANY)],
            out_specs=pl.BlockSpec(memory_space=pltpu.VMEM),
            scratch_shapes=[
                vmem(6, X + 6, Y, Z), vmem(6, Y + 6, X, Z), vmem(6, step + 6, SUB, lines),
                vmem(6, X + 6, Y, Z), vmem(6, Y + 6, X, Z), vmem(6, step + 6, SUB, lines),
                vmem(6, Z, lines), vmem(6, SUB, lines), vmem(6, SUB, lines), vmem(6, SUB, lines),
                vmem(SUB, LANES), vmem(SUB, LANES), vmem(sizes[0] - 1, SUB, LANES), vmem(others, SUB, LANES),
                vmem(SUB, LANES),
                vmem(3, lines, Z), vmem(2, lines, Z), vmem(Z, lines),
                vmem(X + 2, Y, Z), vmem(Y + 2, X, Z), vmem(step + 2, SUB, lines),
                vmem(SUB, lines), vmem(SUB, lines), vmem(SUB, lines),
                vmem(6, lines, Z), vmem(6, lines, Z), vmem(6, Z, lines),
                dma, dma((14,)), dma((14,)),
                dma((sizes[0] - 1,)), dma((sizes[0] - 1,)), dma((others,)), dma((others,)),
            ],
            compiler_params=pltpu.CompilerParams(collective_id=0, has_side_effects=True),
        )(q)

    placed = P(None, "gx", "gy", "gz")
    return jax.shard_map(per_device, mesh=mesh, in_specs=(placed,), out_specs=placed, check_vma=False)
```

time: 100 us -> 20 us (0.20)
  blocking collectives: 39.9 us -> 0 us
  other arithmetic: 26.2 us -> 0 us
  Pallas kernels: 0 us -> 18 us
  waiting for transfers between devices: 13.2 us -> 0 us
  local copies, waits for them, and re-layouts: 10.7 us -> 1.78 us
  starting transfers between devices: 8.74 us -> 0 us
  between operations: 1.02 us -> 0.01 us
    pmax x1 -> x0, blocking collectives: 39.9 us -> none  [per_device(): top_speed = lax.pmax(jnp.max(wave_speed(fluid_state)), ('gx', 'gy', 'gz'))]
    pallas_call x0 -> x1, Pallas kernels: none -> 18 us  [per_device(): pl.pallas_call(functools.partial(kernel, sizes), name='section', out_shap...]
    ppermute x6 -> x0, waiting for transfers between devices: 13.2 us -> none  [the longest x3 6.71 us: padded_2(): lax.ppermute(lax.slice_in_dim(block, 0, width, axis=dim), axis, backward)]
    add x4 -> x0, other arithmetic: 10.7 us -> none  [the longest x3 9.67 us: flux_tendency(): face_flux + weno_face(shifted(minus_part, 3), shifted(minus_part, 2), shi...]
    ppermute x6 -> x0, starting transfers between devices: 8.74 us -> none  [the longest x3 7.6 us: padded_2(): lax.ppermute(lax.slice_in_dim(block, 0, width, axis=dim), axis, backward)]
    slice x6 -> x0, local copies, waits for them, and re-layouts: 6.38 us -> none  [the longest x2 3.59 us: padded_2(): lax.slice_in_dim(block, 0, width, axis=dim)]
    mul x4 -> x0, other arithmetic: 5.23 us -> none  [the longest x3 5.07 us: flux_tendency(): plus_part = 0.5 * (flux_whole + top_speed * conserved)]
    unnamed x15 -> x0, other arithmetic: 4.11 us -> none
  transfers between devices with their start and end apart: 6 -> 0, of which waited for: 6 -> 0; matrix products, arithmetic and copies ran while one was open for 5% -> 0% of each run, Pallas kernels for 0% -> 0%
where the time goes in v1:
time: 20 us; the launch traced here: 19.8 us
  Pallas kernels  18 us (90%)
  local copies, waits for them, and re-layouts  1.78 us (9%)
    pallas_call x1, Pallas kernels, per_device(): pl.pallas_call(functools.partial(kernel, sizes), name='section', out_shap...  18 us
    unnamed x1, local copies, waits for them, and re-layouts  1.78 us

profile of v1, /device:TPU:0, one launch (start us, length us, event | category | flops | bytes accessed | tf_op | source)
XLA Modules:
  0.0 19.8 jit_solution(15761067429725168450)
XLA Ops:
  0.0 18.0 %section.1 = f32[6,8,16,128]{3,2,1,0:T(8,128)} custom-call(f32[6,8,16,128]{3,2,1,0:T(8,128)} %q_hbm.1), custom_call_target="tpu_custom_call" | custom-call | tf_op jit(solution)/shard_map/section/pallas_call | solution.py:385
  18.0 1.8 %copy.3 = f32[6,8,16,128]{3,2,1,0:T(8,128)} copy(f32[6,8,16,128]{3,2,1,0:T(8,128)} %section.1) | data formatting | bytes 786432

commit v2 on v1

--- a/solution.py
+++ b/solution.py
@@ -83,6 +83,15 @@
     return [faces[i + 1] - faces[i] for i in range(len(faces) - 1)]
 
 
+def rounds(sizes):
+    x, y, z = sizes
+    plane = [(0, a, b) for a in range(y) for b in range(z)][1:]
+    line = [(a, 0, 0) for a in range(1, x)]
+    if x * y * z > 64:
+        return line, plane
+    return [(a, b, c) for a in range(x) for b in range(y) for c in range(z)][1:], []
+
+
 def kernel(sizes, q_hbm, out_ref, px, py, pz, fx, fy, fz, tq, zsend, zleft, zright, ts0, ts1, tsa, tsb, speed_ref,
            gb, nb, tb, nxp, nyp, nzp, nzsend, nzleft, nzright, src, ay, tz,
            local_sem, send_sem, recv_sem, sa_sem, ra_sem, sb_sem, rb_sem):
@@ -91,7 +100,7 @@
     step = Z // SUB
     lines = X * Y
     ix, iy, iz = lax.axis_index("gx"), lax.axis_index("gy"), lax.axis_index("gz")
-    offsets_b = [(a, b) for a in range(ngy) for b in range(ngz) if (a, b) != (0, 0)]
+    offsets_a, offsets_b = rounds(sizes)
 
     load = pltpu.make_async_copy(q_hbm, px.at[:, 3 : 3 + X], local_sem)
     load.start()
@@ -103,10 +112,11 @@
     def peer_yz(a, b):
         return {"gy": lax.rem(iy + a + ngy, ngy), "gz": lax.rem(iz + b + ngz, ngz)}
 
-    for offset in range(1, ngx):
-        pl.semaphore_signal(barrier, inc=1, device_id=peer_x(offset), device_id_type=MESH)
-    for a, b in offsets_b:
-        pl.semaphore_signal(barrier, inc=1, device_id=peer_yz(a, b), device_id_type=MESH)
+    def peer(offset):
+        return {**peer_x(offset[0]), **peer_yz(offset[1], offset[2])}
+
+    for offset in offsets_a + offsets_b:
+        pl.semaphore_signal(barrier, inc=1, device_id=peer(offset), device_id_type=MESH)
 
     row = lax.broadcasted_iota(jnp.int32, (SUB, LANES), 0)
     pxf = px.reshape(6 * (X + 6) * Y, LANES)
@@ -128,18 +138,8 @@
             top = jnp.maximum(jnp.maximum(jnp.abs(u[0]), jnp.abs(u[1])), jnp.abs(u[2]))
             top = top + jnp.sqrt(gamma_gas * p * inverse)
             best = top if best is None else jnp.maximum(best, top)
-    ts0[...] = best
-
-    def lay_out(c, carry):
-        for y in range(Y):
-            py[c, 3 + y] = pxf[rows_y((c * (X + 6) + 3) * Y, y), :]
-        turned = px[c, 3 : 3 + X].reshape(lines, Z).T
-        tq[c] = turned
-        zsend[c] = jnp.where(row < 4, turned[:SUB], turned[Z - SUB :])
-        return carry
-
-    lax.fori_loop(0, 6, lay_out, 0)
-    pl.semaphore_wait(barrier, ngx - 1 + len(offsets_b))
+    ts0[...] = jnp.max(best, axis=0, keepdims=True)
+    pl.semaphore_wait(barrier, len(offsets_a) + len(offsets_b))
 
     def remote(source, target, index, peer, sends=send_sem, recvs=recv_sem):
         copy = pltpu.make_async_remote_copy(
@@ -149,13 +149,27 @@
         copy.start()
         return copy
 
-    reduce_a = [remote(ts0, tsa.at[o - 1], o - 1, peer_x(o), sa_sem, ra_sem) for o in range(1, ngx)]
+    reduce_a = [remote(ts0, tsa.at[o], o, peer(offset), sa_sem, ra_sem) for o, offset in enumerate(offsets_a)]
     xlow, xhigh, ilow, ihigh = pl.ds(0, 3), pl.ds(3 + X, 3), pl.ds(3, 3), pl.ds(X, 3)
     first, rest = pl.ds(0, 2), pl.ds(2, 4)
     halo_x0 = [
         remote(px.at[first, ihigh], px.at[first, xlow], 0, peer_x(1)),
         remote(px.at[first, ilow], px.at[first, xhigh], 1, peer_x(-1)),
     ]
+    halo_x1 = [
+        remote(px.at[rest, ihigh], px.at[rest, xlow], 6, peer_x(1)),
+        remote(px.at[rest, ilow], px.at[rest, xhigh], 7, peer_x(-1)),
+    ]
+
+    def lay_out(c, carry):
+        for y in range(Y):
+            py[c, 3 + y] = pxf[rows_y((c * (X + 6) + 3) * Y, y), :]
+        turned = px[c, 3 : 3 + X].reshape(lines, Z).T
+        tq[c] = turned
+        zsend[c] = jnp.where(row < 4, turned[:SUB], turned[Z - SUB :])
+        return carry
+
+    lax.fori_loop(0, 6, lay_out, 0)
     halo_z = [remote(zsend, zleft, 2, peer_yz(0, 1))]
     if ngz > 2:
         halo_z.append(remote(zsend, zright, 3, peer_yz(0, -1)))
@@ -166,10 +180,6 @@
         remote(py.at[:, pl.ds(Y, 3)], py.at[:, pl.ds(0, 3)], 4, peer_yz(1, 0)),
         remote(py.at[:, pl.ds(3, 3)], py.at[:, pl.ds(3 + Y, 3)], 5, peer_yz(-1, 0)),
     ]
-    halo_x1 = [
-        remote(px.at[rest, ihigh], px.at[rest, xlow], 6, peer_x(1)),
-        remote(px.at[rest, ilow], px.at[rest, xhigh], 7, peer_x(-1)),
-    ]
 
     def fill_z(c, carry):
         for b in range(step):
@@ -203,17 +213,13 @@
 
     lax.fori_loop(0, X // 2, inner_x, 0)
 
-    for copy in reduce_a:
-        copy.wait()
-    best = ts0[...]
-    for o in range(ngx - 1):
-        best = jnp.maximum(best, tsa[o])
-    ts1[...] = best
-
     lax.fori_loop(0, Y // 2, inner_yz, 0)
-    reduce_b = [
-        remote(ts1, tsb.at[o], o, peer_yz(*offsets_b[o]), sb_sem, rb_sem) for o in range(len(offsets_b))
-    ]
+    reduce_b = []
+    if offsets_b:
+        for copy in reduce_a:
+            copy.wait()
+        ts1[...] = jnp.maximum(ts0[...], jnp.max(tsa[...], axis=0))
+        reduce_b = [remote(ts1, tsb.at[o], o, peer(offset), sb_sem, rb_sem) for o, offset in enumerate(offsets_b)]
 
     def colour(q0, q1):
         return q0 / (q0 + q1)
@@ -285,12 +291,10 @@
         flux_of(py, fy, 1, s)
         flux_of(py, fy, 1, 3 + Y + s)
 
-    for copy in reduce_b:
-        copy.wait()
-    best = ts1[...]
-    for o in range(len(offsets_b)):
-        best = jnp.maximum(best, tsb[o])
-    best = jnp.max(jnp.max(best, axis=1, keepdims=True), axis=0, keepdims=True)
+    for copy in reduce_b if offsets_b else reduce_a:
+        copy.wait()
+    mine, others = (ts1, tsb) if offsets_b else (ts0, tsa)
+    best = jnp.max(jnp.maximum(mine[...], jnp.max(others[...], axis=0)), axis=1, keepdims=True)
     speed_ref[...] = jnp.broadcast_to(best, (SUB, LANES))
 
     def sweep_z(c, carry):
@@ -370,7 +374,7 @@
 
 def solution(mesh):
     sizes = tuple(mesh.shape[name] for name in ("gx", "gy", "gz"))
-    others = sizes[1] * sizes[2] - 1
+    count_a, count_b = (max(len(offsets), 1) for offsets in rounds(sizes))
 
     def per_device(q):
         _, X, Y, Z = q.shape
@@ -385,24 +389,24 @@
         return pl.pallas_call(
             functools.partial(kernel, sizes),
             name="section",
-            out_shape=jax.ShapeDtypeStruct(q.shape, F32),
-            in_specs=[pl.BlockSpec(memory_space=pl.ANY)],
+            out_shape=pltpu.VMEM(q.shape, F32),
+            in_specs=[pl.BlockSpec(memory_space=pltpu.HBM)],
             out_specs=pl.BlockSpec(memory_space=pltpu.VMEM),
             scratch_shapes=[
                 vmem(6, X + 6, Y, Z), vmem(6, Y + 6, X, Z), vmem(6, step + 6, SUB, lines),
                 vmem(6, X + 6, Y, Z), vmem(6, Y + 6, X, Z), vmem(6, step + 6, SUB, lines),
                 vmem(6, Z, lines), vmem(6, SUB, lines), vmem(6, SUB, lines), vmem(6, SUB, lines),
-                vmem(SUB, LANES), vmem(SUB, LANES), vmem(sizes[0] - 1, SUB, LANES), vmem(others, SUB, LANES),
+                vmem(1, LANES), vmem(1, LANES), vmem(count_a, 1, LANES), vmem(count_b, 1, LANES),
                 vmem(SUB, LANES),
                 vmem(3, lines, Z), vmem(2, lines, Z), vmem(Z, lines),
                 vmem(X + 2, Y, Z), vmem(Y + 2, X, Z), vmem(step + 2, SUB, lines),
                 vmem(SUB, lines), vmem(SUB, lines), vmem(SUB, lines),
                 vmem(6, lines, Z), vmem(6, lines, Z), vmem(6, Z, lines),
                 dma, dma((14,)), dma((14,)),
-                dma((sizes[0] - 1,)), dma((sizes[0] - 1,)), dma((others,)), dma((others,)),
+                dma((count_a,)), dma((count_a,)), dma((count_b,)), dma((count_b,)),
             ],
-            compiler_params=pltpu.CompilerParams(collective_id=0, has_side_effects=True),
-        )(q)
+            compiler_params=pltpu.CompilerParams(collective_id=0, has_side_effects=True, vmem_limit_bytes=24 * 2**20),
+        )(pltpu.with_memory_space_constraint(q, pltpu.HBM))
 
     placed = P(None, "gx", "gy", "gz")
     return jax.shard_map(per_device, mesh=mesh, in_specs=(placed,), out_specs=placed, check_vma=False)

time: 20 us -> 21 us (1.050)
  Pallas kernels: 18 us -> 20.1 us
  local copies, waits for them, and re-layouts: 1.78 us -> 0.75 us
    pallas_call x1, Pallas kernels: 18 us -> 20.1 us  [per_device(): pl.pallas_call(functools.partial(kernel, sizes), name='section', out_shap...]
    unnamed x1, local copies, waits for them, and re-layouts: 1.78 us -> 0.75 us
where the time goes in v2:
time: 21 us; the launch traced here: 20.9 us
  Pallas kernels  20.1 us (96%)
  local copies, waits for them, and re-layouts  0.75 us (4%)
    pallas_call x1, Pallas kernels, per_device(): pl.pallas_call(functools.partial(kernel, sizes), name='section', out_shap...  20.1 us
    unnamed x1, local copies, waits for them, and re-layouts  0.75 us

profile of v2, /device:TPU:0, one launch (start us, length us, event | category | flops | bytes accessed | tf_op | source)
XLA Modules:
  0.0 20.9 jit_solution(16445967363646552335)
XLA Ops:
  0.0 20.1 %section.1 = f32[6,8,16,128]{3,2,1,0:T(8,128)S(1)} custom-call(f32[6,8,16,128]{3,2,1,0:T(8,128)} %q_hbm.1), custom_call_target="tpu_custom_call" | custom-call | tf_op jit(solution)/shard_map/section/pallas_call | solution.py:389
  20.1 0.7 %copy.3 = f32[6,8,16,128]{3,2,1,0:T(8,128)} copy(f32[6,8,16,128]{3,2,1,0:T(8,128)S(1)} %section.1) | data formatting | bytes 786432

commit v3 on v2

--- a/solution.py
+++ b/solution.py
@@ -85,15 +85,11 @@
 
 def rounds(sizes):
     x, y, z = sizes
-    plane = [(0, a, b) for a in range(y) for b in range(z)][1:]
-    line = [(a, 0, 0) for a in range(1, x)]
-    if x * y * z > 64:
-        return line, plane
-    return [(a, b, c) for a in range(x) for b in range(y) for c in range(z)][1:], []
+    return [(a, 0, 0) for a in range(1, x)], [(0, a, b) for a in range(y) for b in range(z)][1:]
 
 
 def kernel(sizes, q_hbm, out_ref, px, py, pz, fx, fy, fz, tq, zsend, zleft, zright, ts0, ts1, tsa, tsb, speed_ref,
-           gb, nb, tb, nxp, nyp, nzp, nzsend, nzleft, nzright, src, ay, tz,
+           gb, nb, tb, nxp, nyp, nzp, nzsend, nzleft, nzright, ay, tz,
            local_sem, send_sem, recv_sem, sa_sem, ra_sem, sb_sem, rb_sem):
     ngx, ngy, ngz = sizes
     X, Y, Z = px.shape[1] - 6, px.shape[2], px.shape[3]
@@ -161,25 +157,35 @@
         remote(px.at[rest, ilow], px.at[rest, xhigh], 7, peer_x(-1)),
     ]
 
-    def lay_out(c, carry):
+    def lay_out_y(c, carry):
         for y in range(Y):
             py[c, 3 + y] = pxf[rows_y((c * (X + 6) + 3) * Y, y), :]
+        return carry
+
+    lax.fori_loop(0, 6, lay_out_y, 0)
+    halo_y = [
+        remote(py.at[:, pl.ds(Y, 3)], py.at[:, pl.ds(0, 3)], 4, peer_yz(1, 0)),
+        remote(py.at[:, pl.ds(3, 3)], py.at[:, pl.ds(3 + Y, 3)], 5, peer_yz(-1, 0)),
+    ]
+
+    def lay_out_z(c, carry):
         turned = px[c, 3 : 3 + X].reshape(lines, Z).T
         tq[c] = turned
         zsend[c] = jnp.where(row < 4, turned[:SUB], turned[Z - SUB :])
         return carry
 
-    lax.fori_loop(0, 6, lay_out, 0)
+    lax.fori_loop(0, 6, lay_out_z, 0)
     halo_z = [remote(zsend, zleft, 2, peer_yz(0, 1))]
     if ngz > 2:
         halo_z.append(remote(zsend, zright, 3, peer_yz(0, -1)))
         from_right = zright
     else:
         from_right = zleft
-    halo_y = [
-        remote(py.at[:, pl.ds(Y, 3)], py.at[:, pl.ds(0, 3)], 4, peer_yz(1, 0)),
-        remote(py.at[:, pl.ds(3, 3)], py.at[:, pl.ds(3 + Y, 3)], 5, peer_yz(-1, 0)),
-    ]
+
+    for copy in reduce_a:
+        copy.wait_recv()
+    ts1[...] = jnp.maximum(ts0[...], jnp.max(tsa[...], axis=0))
+    reduce_b = [remote(ts1, tsb.at[o], o, peer(offset), sb_sem, rb_sem) for o, offset in enumerate(offsets_b)]
 
     def fill_z(c, carry):
         for b in range(step):
@@ -214,19 +220,12 @@
     lax.fori_loop(0, X // 2, inner_x, 0)
 
     lax.fori_loop(0, Y // 2, inner_yz, 0)
-    reduce_b = []
-    if offsets_b:
-        for copy in reduce_a:
-            copy.wait()
-        ts1[...] = jnp.maximum(ts0[...], jnp.max(tsa[...], axis=0))
-        reduce_b = [remote(ts1, tsb.at[o], o, peer(offset), sb_sem, rb_sem) for o, offset in enumerate(offsets_b)]
-
     def colour(q0, q1):
         return q0 / (q0 + q1)
 
     central = 1.0 / (2.0 * spacing)
     for copy in halo_z:
-        copy.wait()
+        copy.wait_recv()
 
     def join_z(c, carry):
         for s in range(3):
@@ -248,14 +247,14 @@
         flux_of(pz, fz, 2, 3 + step + s)
 
     for copy in halo_y:
-        copy.wait()
+        copy.wait_recv()
     colours = [colour(py[0, 2 + y], py[1, 2 + y]) for y in range(Y + 2)]
     gbf = gb.reshape(3 * lines, LANES)
     for y in range(Y):
         gbf[rows_y(lines, y), :] = (colours[y + 2] - colours[y]) * central
 
     for copy in halo_x0:
-        copy.wait()
+        copy.wait_recv()
     for half in range(halves):
         part = pl.ds(half * SUB, SUB)
         colours = [colour(px[0, 2 + x, part, :], px[1, 2 + x, part, :]) for x in range(X + 2)]
@@ -291,10 +290,9 @@
         flux_of(py, fy, 1, s)
         flux_of(py, fy, 1, 3 + Y + s)
 
-    for copy in reduce_b if offsets_b else reduce_a:
-        copy.wait()
-    mine, others = (ts1, tsb) if offsets_b else (ts0, tsa)
-    best = jnp.max(jnp.maximum(mine[...], jnp.max(others[...], axis=0)), axis=1, keepdims=True)
+    for copy in reduce_b:
+        copy.wait_recv()
+    best = jnp.max(jnp.maximum(ts1[...], jnp.max(tsb[...], axis=0)), axis=1, keepdims=True)
     speed_ref[...] = jnp.broadcast_to(best, (SUB, LANES))
 
     def sweep_z(c, carry):
@@ -318,35 +316,8 @@
     lax.fori_loop(0, 6, sweep_z, 0)
     lax.fori_loop(0, 6, sweep_y, 0)
 
-    for copy in normals:
-        copy.wait()
-    left = jnp.broadcast_to(nzleft[pl.ds(SUB - 1, 1), :], (SUB, LANES))
-    nzp[0] = jnp.where(row == 0, left, pltpu.roll(nzp[step], 1, 0))
-    right = jnp.broadcast_to(normal_right[pl.ds(0, 1), :], (SUB, LANES))
-    nzp[1 + step] = jnp.where(row == SUB - 1, right, pltpu.roll(nzp[1], SUB - 1, 0))
-    for b in range(step):
-        tb[rows_z(0, b), :] = nzp[b + 2] - nzp[b]
-    nb[1] = tb[...].T
-    for y in range(Y):
-        nbf[rows_y(0, y), :] = nyp[y + 2] - nyp[y]
-    zero = jnp.zeros((SUB, LANES), F32)
-    for x in range(X):
-        for half in range(halves):
-            part = pl.ds(half * SUB, SUB)
-            at = pl.ds(x * Y + half * SUB, SUB)
-            q = [px[c, 3 + x, part, :] for c in range(5)]
-            inverse = 1.0 / (q[0] + q[1])
-            along = (nxp[x + 2, part, :] - nxp[x, part, :]) + nb[0, at, :] + nb[1, at, :]
-            pull = (-tension * central) * along
-            force = [pull * gb[k, at, :] for k in range(3)]
-            src[0, at, :] = zero
-            src[1, at, :] = zero
-            for k in range(3):
-                src[2 + k, at, :] = force[k]
-            src[5, at, :] = (force[0] * q[2] + force[1] * q[3] + force[2] * q[4]) * inverse
-
     for copy in halo_x1:
-        copy.wait()
+        copy.wait_recv()
     for s in range(3):
         flux_x(s)
         flux_x(3 + X + s)
@@ -366,10 +337,39 @@
                 start = x * Y + half * SUB
                 at = pl.ds(start, SUB)
                 change = parts[x] + ay[c, at, :] + back[start : start + SUB]
-                out_ref[c, x, part, :] = state[3 + x] + (slope * change + timestep * src[c, at, :])
+                out_ref[c, x, part, :] = state[3 + x] + slope * change
         return carry
 
     lax.fori_loop(0, 6, sweep_x, 0)
+
+    for copy in normals:
+        copy.wait_recv()
+    left = jnp.broadcast_to(nzleft[pl.ds(SUB - 1, 1), :], (SUB, LANES))
+    nzp[0] = jnp.where(row == 0, left, pltpu.roll(nzp[step], 1, 0))
+    right = jnp.broadcast_to(normal_right[pl.ds(0, 1), :], (SUB, LANES))
+    nzp[1 + step] = jnp.where(row == SUB - 1, right, pltpu.roll(nzp[1], SUB - 1, 0))
+    for b in range(step):
+        tb[rows_z(0, b), :] = nzp[b + 2] - nzp[b]
+    nb[1] = tb[...].T
+    for y in range(Y):
+        nbf[rows_y(0, y), :] = nyp[y + 2] - nyp[y]
+    timestep = (courant * spacing) / (3.0 * speed_ref[...])
+    for x in range(X):
+        for half in range(halves):
+            part = pl.ds(half * SUB, SUB)
+            at = pl.ds(x * Y + half * SUB, SUB)
+            q = [px[c, 3 + x, part, :] for c in range(5)]
+            inverse = 1.0 / (q[0] + q[1])
+            along = (nxp[x + 2, part, :] - nxp[x, part, :]) + nb[0, at, :] + nb[1, at, :]
+            pull = ((-tension * central) * along) * timestep
+            force = [pull * gb[k, at, :] for k in range(3)]
+            for k in range(3):
+                out_ref[2 + k, x, part, :] += force[k]
+            out_ref[5, x, part, :] += (force[0] * q[2] + force[1] * q[3] + force[2] * q[4]) * inverse
+
+    for copies in (reduce_a, reduce_b, halo_x0, halo_x1, halo_y, halo_z, normals):
+        for copy in copies:
+            copy.wait_send()
 
 
 def solution(mesh):
@@ -401,7 +401,7 @@
                 vmem(3, lines, Z), vmem(2, lines, Z), vmem(Z, lines),
                 vmem(X + 2, Y, Z), vmem(Y + 2, X, Z), vmem(step + 2, SUB, lines),
                 vmem(SUB, lines), vmem(SUB, lines), vmem(SUB, lines),
-                vmem(6, lines, Z), vmem(6, lines, Z), vmem(6, Z, lines),
+                vmem(6, lines, Z), vmem(6, Z, lines),
                 dma, dma((14,)), dma((14,)),
                 dma((count_a,)), dma((count_a,)), dma((count_b,)), dma((count_b,)),
             ],

time: 21 us -> 17.3 us (0.82)
  Pallas kernels: 20.1 us -> 16.4 us
    pallas_call x1, Pallas kernels: 20.1 us -> 16.4 us  [per_device(): pl.pallas_call(functools.partial(kernel, sizes), name='section', out_shap...]
where the time goes in v3:
time: 17.3 us; the launch traced here: 17.2 us
  Pallas kernels  16.4 us (95%)
  local copies, waits for them, and re-layouts  0.75 us (4%)
    pallas_call x1, Pallas kernels, per_device(): pl.pallas_call(functools.partial(kernel, sizes), name='section', out_shap...  16.4 us
    unnamed x1, local copies, waits for them, and re-layouts  0.75 us

profile of v3, /device:TPU:0, one launch (start us, length us, event | category | flops | bytes accessed | tf_op | source)
XLA Modules:
  0.0 17.2 jit_solution(8283107388757773251)
XLA Ops:
  0.0 16.4 %section.1 = f32[6,8,16,128]{3,2,1,0:T(8,128)S(1)} custom-call(f32[6,8,16,128]{3,2,1,0:T(8,128)} %q_hbm.1), custom_call_target="tpu_custom_call" | custom-call | tf_op jit(solution)/shard_map/section/pallas_call | solution.py:389
  16.4 0.7 %copy.3 = f32[6,8,16,128]{3,2,1,0:T(8,128)} copy(f32[6,8,16,128]{3,2,1,0:T(8,128)S(1)} %section.1) | data formatting | bytes 786432

commit v4 on v3

--- a/solution.py
+++ b/solution.py
@@ -16,7 +16,7 @@
 
 MESH = pl.DeviceIdType.MESH
 SUB, LANES = 8, 128
-SCALE = 0.25
+SCALE = 0.125
 F32 = jnp.float32
 
 
@@ -35,8 +35,7 @@
     return out
 
 
-def correction(e0, e1, e2, third_a, third_b):
-    q0, q1, q2 = e0 * e0, e1 * e1, e2 * e2
+def correction(q0, q1, q2, third_a, third_b):
     a = q1 * q2
     b = 3.0 * (q0 * q1)
     total = a + (b + 6.0 * (q0 * q2))
@@ -46,39 +45,34 @@
 def differences(v):
     n = len(v)
     d = [v[i + 1] - v[i] for i in range(n - 1)]
-    h = [None] + [0.5 * (d[i] - d[i - 1]) for i in range(1, n - 1)]
-    e = [None] + [h[i] * h[i] * (13.0 / 3.0) + weno_eps * SCALE * SCALE for i in range(1, n - 1)]
-    j = [None, None] + [(2.0 / 3.0) * (h[i] - h[i - 1]) for i in range(2, n - 1)]
-    return d, h, e, j
-
-
-def square(value):
-    return value * value
+    second, middle, up, down = [None], [None], [None], [None]
+    for i in range(1, n - 1):
+        bend = d[i] - d[i - 1]
+        slope = d[i] + d[i - 1]
+        bend_4 = 4.0 * bend
+        square, cross = bend_4 * bend, bend_4 * slope
+        e = (slope * slope + 4.0 * weno_eps * SCALE * SCALE) + (13.0 / 12.0) * square
+        base = e + square
+        above, below = base + cross, base - cross
+        second.append(bend)
+        middle.append(e * e)
+        up.append(above * above)
+        down.append(below * below)
+    third = [None, None] + [second[i] - second[i - 1] for i in range(2, n - 1)]
+    return d, second, third, middle, up, down
 
 
 def weno_tendency(flux, state):
     n = len(flux)
     vp = [f + s for f, s in zip(flux, state)]
     vm = [f - s for f, s in zip(flux, state)]
-    d, h, e, j = differences(vp)
-    dm, hm, em, jm = differences(vm)
+    d, h, j, mid, up, down = differences(vp)
+    dm, hm, jm, mid_m, up_m, down_m = differences(vm)
     faces = []
     for i in range(2, n - 3):
-        fix = correction(
-            e[i - 1] + square(d[i - 1] + h[i - 1]),
-            e[i] + square(d[i - 1] + h[i]),
-            e[i + 1] + square(h[i + 1] - d[i]),
-            j[i],
-            0.5 * j[i + 1],
-        )
-        fix_m = correction(
-            em[i + 2] + square(hm[i + 2] - dm[i + 1]),
-            em[i + 1] + square(hm[i + 1] - dm[i + 1]),
-            em[i] + square(hm[i] + dm[i]),
-            jm[i + 2],
-            0.5 * jm[i + 1],
-        )
-        linear = (vp[i] + vm[i + 1]) + 0.5 * (d[i - 1] - dm[i + 1]) + (2.0 / 3.0) * (h[i] + hm[i + 1])
+        fix = correction(up[i - 1], mid[i], down[i + 1], j[i], 0.5 * j[i + 1])
+        fix_m = correction(down_m[i + 2], mid_m[i + 1], up_m[i], jm[i + 2], 0.5 * jm[i + 1])
+        linear = 3.0 * (vp[i] + vm[i + 1]) + 1.5 * (d[i - 1] - dm[i + 1]) + (h[i] + hm[i + 1])
         faces.append(linear + (fix_m - fix))
     return [faces[i + 1] - faces[i] for i in range(len(faces) - 1)]
 
@@ -152,10 +146,6 @@
         remote(px.at[first, ihigh], px.at[first, xlow], 0, peer_x(1)),
         remote(px.at[first, ilow], px.at[first, xhigh], 1, peer_x(-1)),
     ]
-    halo_x1 = [
-        remote(px.at[rest, ihigh], px.at[rest, xlow], 6, peer_x(1)),
-        remote(px.at[rest, ilow], px.at[rest, xhigh], 7, peer_x(-1)),
-    ]
 
     def lay_out_y(c, carry):
         for y in range(Y):
@@ -186,6 +176,11 @@
         copy.wait_recv()
     ts1[...] = jnp.maximum(ts0[...], jnp.max(tsa[...], axis=0))
     reduce_b = [remote(ts1, tsb.at[o], o, peer(offset), sb_sem, rb_sem) for o, offset in enumerate(offsets_b)]
+
+    halo_x1 = [
+        remote(px.at[rest, ihigh], px.at[rest, xlow], 6, peer_x(1)),
+        remote(px.at[rest, ilow], px.at[rest, xhigh], 7, peer_x(-1)),
+    ]
 
     def fill_z(c, carry):
         for b in range(step):
@@ -326,7 +321,7 @@
         top = speed_ref[...]
         scaled = (0.5 * SCALE) * top
         timestep = (courant * spacing) / (3.0 * top)
-        slope = timestep * (-1.0 / (spacing * SCALE))
+        slope = timestep * (-1.0 / (3.0 * spacing * SCALE))
         count = X + 6
         back = tz[c].T
         for half in range(halves):

time: 17.3 us -> 17.2 us (level)
  no operation moved by 1% of the time
where the time goes in v4:
time: 17.2 us; the launch traced here: 17 us
  Pallas kernels  16.3 us (95%)
  local copies, waits for them, and re-layouts  0.75 us (4%)
    pallas_call x1, Pallas kernels, per_device(): pl.pallas_call(functools.partial(kernel, sizes), name='section', out_shap...  16.3 us
    unnamed x1, local copies, waits for them, and re-layouts  0.75 us

profile of v4, /device:TPU:0, one launch (start us, length us, event | category | flops | bytes accessed | tf_op | source)
XLA Modules:
  0.0 17.0 jit_solution(14140764591353251753)
XLA Ops:
  0.0 16.3 %section.1 = f32[6,8,16,128]{3,2,1,0:T(8,128)S(1)} custom-call(f32[6,8,16,128]{3,2,1,0:T(8,128)} %q_hbm.1), custom_call_target="tpu_custom_call" | custom-call | tf_op jit(solution)/shard_map/section/pallas_call | solution.py:384
  16.3 0.7 %copy.3 = f32[6,8,16,128]{3,2,1,0:T(8,128)} copy(f32[6,8,16,128]{3,2,1,0:T(8,128)S(1)} %section.1) | data formatting | bytes 786432
